TPU v7x, 32 devices: a whole 2x2x4 slice. The times are simulated.
32 devices in a mesh: gx: 4 (over y, core), gy: 8 (over z, x).
Axes of the slice: x: 2, y: 2, z: 4, core: 2. Of those that a mesh axis runs over, the one named last changes fastest.
Arguments:
- source: float32 [64, 16, 1024], P(None, 'gx', 'gy'), may hold values from -6 to 6
- initial: float32 [64, 16, 1024], P(None, 'gx', 'gy'), may hold values from -6 to 6
- reaction: float32 [64, 16, 1024], P(None, 'gx', 'gy'), may hold values from 1 to 3
- stiffness: float32 [16, 1024], P('gx', 'gy'), may hold values from 0.5 to 2
- line_op: float32 [8, 8], replicated, may hold values from -1.6 to 5.6
- face_deriv: float32 [8], replicated, may hold values from -2 to 2
- wall_flags: int32 [4, 16, 1024], P(None, 'gx', 'gy'), may hold values 0 or 1
Outputs:
- hessenberg: float32 [6, 5], replicated
- krylov_basis: float32 [6, 64, 16, 1024], P(None, None, 'gx', 'gy')
All inputs are finite; a program needn't handle non-finite values. No bound on the sum of `wall_flags` on one device may be relied on, other than what follows from the above.
Results may differ from a plain program's by a relative error of at most 0.0003.
Values sent between devices are 32-bit elements; how exact they have to be, the bound alone decides.
A program may use at most 64 MiB of HBM per device.

v0:
```python
import jax
import jax.numpy as jnp
from jax import lax
from jax.sharding import PartitionSpec as P

P_SIZE = 8
ITERS = 5
TAU = 2.0
FLOOR = 0.1


def extended(array, sides, width):
    for axis, dim in sides:
        devices, length = (lax.axis_size(axis), array.shape[dim])
        up = [(i, (i + 1) % devices) for i in range(devices)]
        down = [(j, i) for i, j in up]
        last = lax.slice_in_dim(array, length - width, length, axis=dim)
        leading = lax.slice_in_dim(array, 0, width, axis=dim)
        before = lax.ppermute(last, axis, up)
        after = lax.ppermute(leading, axis, down)
        array = jnp.concatenate([before, array, after], axis=dim)
    return array


def local_total(values):
    return jnp.sum(jnp.sum(values, axis=0))


def x_traces(nodes, face_deriv):
    highest = lax.Precision.HIGHEST
    lower = jnp.einsum("c,cbxy->bxy", face_deriv, nodes, precision=highest)
    upper = jnp.einsum("c,cbxy->bxy", face_deriv[::-1], nodes, precision=highest)
    return jnp.stack([nodes[0], lower, nodes[-1], upper])


def y_traces(nodes, face_deriv):
    highest = lax.Precision.HIGHEST
    lower = jnp.einsum("c,acxy->axy", face_deriv, nodes, precision=highest)
    upper = jnp.einsum("c,acxy->axy", face_deriv[::-1], nodes, precision=highest)
    return jnp.stack([nodes[:, 0], lower, nodes[:, -1], upper])


def apply_op(field, reaction, stiffness, line_op, face_deriv, opened):
    highest = lax.Precision.HIGHEST
    nodes = field.reshape(P_SIZE, P_SIZE, field.shape[1], field.shape[2])
    interior = stiffness * (
        jnp.einsum("ac,cbxy->abxy", line_op, nodes, precision=highest)
        + jnp.einsum("bc,acxy->abxy", line_op, nodes, precision=highest)
    )
    padded = extended(nodes, (("gx", 2), ("gy", 3)), 1)
    xside = x_traces(padded, face_deriv)[:, :, :, 1:-1]
    yside = y_traces(padded, face_deriv)[:, :, 1:-1, :]
    x_own = xside[:, :, 1:-1]
    y_own = yside[:, :, :, 1:-1]
    east_nb = xside[0:2, :, 2:]
    west_nb = xside[2:4, :, :-2]
    north_nb = yside[0:2, :, :, 2:]
    south_nb = yside[2:4, :, :, :-2]
    add_east = TAU * (x_own[2] - opened[1] * east_nb[0]) + 0.5 * (x_own[3] - opened[1] * east_nb[1])
    add_west = TAU * (x_own[0] - opened[0] * west_nb[0]) + 0.5 * (x_own[1] - opened[0] * west_nb[1])
    add_north = TAU * (y_own[2] - opened[3] * north_nb[0]) + 0.5 * (
        y_own[3] - opened[3] * north_nb[1]
    )
    add_south = TAU * (y_own[0] - opened[2] * south_nb[0]) + 0.5 * (
        y_own[1] - opened[2] * south_nb[1]
    )
    result = reaction.reshape(nodes.shape) * nodes + interior
    result = result.at[0].add(add_west).at[P_SIZE - 1].add(add_east)
    result = result.at[:, 0].add(add_south).at[:, P_SIZE - 1].add(add_north)
    return result.reshape(field.shape)


def norm_scale(vector, total):
    squares = lax.psum(local_total(vector * vector), ("gx", "gy"))
    return jnp.sqrt(squares / total + FLOOR)


def body(source, initial, reaction, stiffness, line_op, face_deriv, wall_flags):
    highest = lax.Precision.HIGHEST
    total = float(
        P_SIZE
        * P_SIZE
        * source.shape[1]
        * lax.axis_size("gx")
        * source.shape[2]
        * lax.axis_size("gy")
    )
    opened = 1.0 - wall_flags.astype(jnp.float32)

    def operate(field):
        return apply_op(field, reaction, stiffness, line_op, face_deriv, opened)

    def products(basis, image):
        per_cell = jnp.einsum("kqxy,qxy->kxy", basis, image, precision=highest)
        return jnp.sum(per_cell, axis=(1, 2))

    first = source - operate(initial)
    basis = jnp.zeros((ITERS + 1,) + source.shape, jnp.float32)
    hessen = jnp.zeros((ITERS + 1, ITERS), jnp.float32)
    rows = lax.broadcasted_iota(jnp.int32, (ITERS + 1, ITERS), 0)
    cols = lax.broadcasted_iota(jnp.int32, (ITERS + 1, ITERS), 1)
    slots = lax.broadcasted_iota(jnp.int32, (ITERS + 1,), 0)

    def advance(step, carry):
        basis, hessen, pending = carry
        image = operate(pending)
        local = products(basis, image)
        projected, crossed, squares = lax.psum(
            (local, local_total(pending * image), local_total(pending * pending)), ("gx", "gy")
        )
        beta = jnp.sqrt(squares / total + FLOOR)
        basis = lax.dynamic_update_index_in_dim(basis, pending / beta, step, 0)
        coeffs = projected / (total * beta) + jnp.where(
            slots == step, crossed / (total * beta * beta), 0.0
        )
        pending = image / beta - jnp.einsum("k,kqxy->qxy", coeffs, basis, precision=highest)
        hessen = hessen + jnp.where(cols == step, coeffs[:, None], 0.0)
        hessen = hessen + jnp.where((rows == step) & (cols == step - 1), beta, 0.0)
        return (basis, hessen, pending)

    basis, hessen, pending = lax.fori_loop(0, ITERS, advance, (basis, hessen, first))
    beta = norm_scale(pending, total)
    basis = basis.at[ITERS].set(pending / beta)
    hessen = hessen + jnp.where((rows == ITERS) & (cols == ITERS - 1), beta, 0.0)
    return (hessen, basis)


def solution(mesh):
    return jax.shard_map(
        body,
        mesh=mesh,
        in_specs=(
            P(None, "gx", "gy"),
            P(None, "gx", "gy"),
            P(None, "gx", "gy"),
            P("gx", "gy"),
            P(),
            P(),
            P(None, "gx", "gy"),
        ),
        out_specs=(P(), P(None, None, "gx", "gy")),
        check_vma=False,
    )
```

profile of v0, /device:TPU:0, one launch (start us, length us, event | category | flops | bytes accessed | tf_op | source)
XLA Modules:
  0.0 408.1 jit_solution(16767970016116543631)
XLA Ops:
  0.6 0.9 copy.257
  2.2 2.0 collective-permute-start.5
  6.0 2.2 collective-permute-start.6
  8.2 3.1 collective-permute-start.7
  12.3 4.8 %collective-permute-done.6 = f32[8,8,6,1]{3,0,2,1:T(8,128)S(1)} collective-permute-done((f32[8,8,6,1]{3,0,2,1:T(8,128)S(1)}, f32[8,8,6,1]{3,0,2,1:T(8,128)S(1)}, u32[]{:S(2)}, u32[]{:S(2)}) %collective-permute-start.6) | collective-permute-done | bytes 1568 | tf_op jit(solution)/shard_map/ppermute | solution.py:19
  17.1 2.8 collective-permute-done.7
  20.9 0.7 fusion.63
  21.6 0.7 fusion.65
  24.3 0.7 copy-done.8
  25.1 0.8 multiply_reduce_fusion.1
  26.0 339.5 %while.31 = (s32[]{:T(128)}, f32[6,64,4,128]{3,2,1,0:T(4,128)S(1)}, f32[6,5]{1,0:T(8,128)S(1)}, f32[64,4,128]{2,1,0:T(4,128)S(1)}, f32[64,4,128]{2,0,1:T(8,128)S...) while((s32[]{:T(128)}, f32[6,64,4,128]{3,2,1,0:T(4,128)S(1)}, ...), condition=%wide.region_6.7_spmd.clone.clone, body=%wide.region_0.6_spmd.clone.clone.sunk | while | flops 14006069 | bytes 9489035 | solution.py:121
  26.3 1.6 collective-permute-start.1
  28.5 1.0 collective-permute-done
  29.6 2.8 collective-permute-start.2
  32.7 4.3 %collective-permute-done.2 = f32[8,8,6,1]{3,0,2,1:T(8,128)S(1)} collective-permute-done((f32[8,8,6,1]{3,0,2,1:T(8,128)S(1)}, f32[8,8,6,1]{3,0,2,1:T(8,128)S(1)}, u32[]{:S(2)}, u32[]{:S(2)}) %collective-permute-start.2) | collective-permute-done | bytes 1568 | tf_op jit(solution)/shard_map/while/body/eval_jaxpr/ppermute | solution.py:20
  37.0 5.2 %collective-permute-done.3 = f32[8,8,6,1]{3,0,2,1:T(8,128)S(1)} collective-permute-done((f32[8,8,6,1]{3,0,2,1:T(8,128)S(1)}, f32[8,8,6,1]{3,0,2,1:T(8,128)S(1)}, u32[]{:S(2)}, u32[]{:S(2)}) %collective-permute-start.3) | collective-permute-done | bytes 1568 | tf_op jit(solution)/shard_map/while/body/eval_jaxpr/ppermute | solution.py:19
  42.4 0.7 fusion.185
  43.1 0.7 fusion.184
  47.3 2.6 convolution_bitcast_fusion.2
  49.8 39.4 %all-reduce.2 = (f32[]{:T(128)}, f32[6]{0:T(128)S(1)}, f32[]{:T(128)}) all-reduce(f32[]{:T(128)} %get-tuple-element.835, f32[6]{0:T(128)S(1)} %convolution_bitcast_fusion.2, f32[]{:T(128)} %fusion.189), channel_id=1, replica_groups=mesh['gx'=4,'gy'=8] {'gx','gy'}, use_global_device_ids=true, to_apply=%region_2.2 | all-reduce | flops 8 | bytes 64 | tf_op jit(solution)/shard_map/while/body/eval_jaxpr/psum | solution.py:108
  90.7 1.4 fusion.191
  92.2 0.8 multiply_reduce_fusion.4
  93.2 1.8 collective-permute-start.1
  95.5 1.0 collective-permute-done
  96.8 3.9 collective-permute-start.2
  101.0 4.9 %collective-permute-done.2 = f32[8,8,6,1]{3,0,2,1:T(8,128)S(1)} collective-permute-done((f32[8,8,6,1]{3,0,2,1:T(8,128)S(1)}, f32[8,8,6,1]{3,0,2,1:T(8,128)S(1)}, u32[]{:S(2)}, u32[]{:S(2)}) %collective-permute-start.2) | collective-permute-done | bytes 1568 | tf_op jit(solution)/shard_map/while/body/eval_jaxpr/ppermute | solution.py:20
  105.9 5.1 %collective-permute-done.3 = f32[8,8,6,1]{3,0,2,1:T(8,128)S(1)} collective-permute-done((f32[8,8,6,1]{3,0,2,1:T(8,128)S(1)}, f32[8,8,6,1]{3,0,2,1:T(8,128)S(1)}, u32[]{:S(2)}, u32[]{:S(2)}) %collective-permute-start.3) | collective-permute-done | bytes 1568 | tf_op jit(solution)/shard_map/while/body/eval_jaxpr/ppermute | solution.py:19
  111.2 0.7 fusion.185
  111.9 0.7 fusion.184
  116.0 2.6 convolution_bitcast_fusion.2
  118.6 39.2 %all-reduce.2 = (f32[]{:T(128)}, f32[6]{0:T(128)S(1)}, f32[]{:T(128)}) all-reduce(f32[]{:T(128)} %get-tuple-element.835, f32[6]{0:T(128)S(1)} %convolution_bitcast_fusion.2, f32[]{:T(128)} %fusion.189), channel_id=1, replica_groups=mesh['gx'=4,'gy'=8] {'gx','gy'}, use_global_device_ids=true, to_apply=%region_2.2 | all-reduce | flops 8 | bytes 64 | tf_op jit(solution)/shard_map/while/body/eval_jaxpr/psum | solution.py:108
  159.3 1.4 fusion.191
  160.8 0.8 multiply_reduce_fusion.4
  161.8 1.8 collective-permute-start.1
  164.1 1.0 collective-permute-done
  165.4 3.9 collective-permute-start.2
  169.6 4.6 %collective-permute-done.2 = f32[8,8,6,1]{3,0,2,1:T(8,128)S(1)} collective-permute-done((f32[8,8,6,1]{3,0,2,1:T(8,128)S(1)}, f32[8,8,6,1]{3,0,2,1:T(8,128)S(1)}, u32[]{:S(2)}, u32[]{:S(2)}) %collective-permute-start.2) | collective-permute-done | bytes 1568 | tf_op jit(solution)/shard_map/while/body/eval_jaxpr/ppermute | solution.py:20
  174.2 4.9 %collective-permute-done.3 = f32[8,8,6,1]{3,0,2,1:T(8,128)S(1)} collective-permute-done((f32[8,8,6,1]{3,0,2,1:T(8,128)S(1)}, f32[8,8,6,1]{3,0,2,1:T(8,128)S(1)}, u32[]{:S(2)}, u32[]{:S(2)}) %collective-permute-start.3) | collective-permute-done | bytes 1568 | tf_op jit(solution)/shard_map/while/body/eval_jaxpr/ppermute | solution.py:19
  179.3 0.7 fusion.185
  180.0 0.7 fusion.184
  184.1 2.6 convolution_bitcast_fusion.2
  186.7 39.1 %all-reduce.2 = (f32[]{:T(128)}, f32[6]{0:T(128)S(1)}, f32[]{:T(128)}) all-reduce(f32[]{:T(128)} %get-tuple-element.835, f32[6]{0:T(128)S(1)} %convolution_bitcast_fusion.2, f32[]{:T(128)} %fusion.189), channel_id=1, replica_groups=mesh['gx'=4,'gy'=8] {'gx','gy'}, use_global_device_ids=true, to_apply=%region_2.2 | all-reduce | flops 8 | bytes 64 | tf_op jit(solution)/shard_map/while/body/eval_jaxpr/psum | solution.py:108
  227.3 1.4 fusion.191
  228.8 0.8 multiply_reduce_fusion.4
  229.7 1.8 collective-permute-start.1
  232.1 1.0 collective-permute-done
  233.3 3.9 collective-permute-start.2
  237.6 4.6 %collective-permute-done.2 = f32[8,8,6,1]{3,0,2,1:T(8,128)S(1)} collective-permute-done((f32[8,8,6,1]{3,0,2,1:T(8,128)S(1)}, f32[8,8,6,1]{3,0,2,1:T(8,128)S(1)}, u32[]{:S(2)}, u32[]{:S(2)}) %collective-permute-start.2) | collective-permute-done | bytes 1568 | tf_op jit(solution)/shard_map/while/body/eval_jaxpr/ppermute | solution.py:20
  242.1 4.9 %collective-permute-done.3 = f32[8,8,6,1]{3,0,2,1:T(8,128)S(1)} collective-permute-done((f32[8,8,6,1]{3,0,2,1:T(8,128)S(1)}, f32[8,8,6,1]{3,0,2,1:T(8,128)S(1)}, u32[]{:S(2)}, u32[]{:S(2)}) %collective-permute-start.3) | collective-permute-done | bytes 1568 | tf_op jit(solution)/shard_map/while/body/eval_jaxpr/ppermute | solution.py:19
  252.1 2.6 convolution_bitcast_fusion.2
  254.7 39.1 %all-reduce.2 = (f32[]{:T(128)}, f32[6]{0:T(128)S(1)}, f32[]{:T(128)}) all-reduce(f32[]{:T(128)} %get-tuple-element.835, f32[6]{0:T(128)S(1)} %convolution_bitcast_fusion.2, f32[]{:T(128)} %fusion.189), channel_id=1, replica_groups=mesh['gx'=4,'gy'=8] {'gx','gy'}, use_global_device_ids=true, to_apply=%region_2.2 | all-reduce | flops 8 | bytes 64 | tf_op jit(solution)/shard_map/while/body/eval_jaxpr/psum | solution.py:108
  295.2 1.4 fusion.191
  296.7 0.8 multiply_reduce_fusion.4
  297.7 1.8 collective-permute-start.1
  300.1 1.0 collective-permute-done
  301.3 3.9 collective-permute-start.2
  305.5 4.6 %collective-permute-done.2 = f32[8,8,6,1]{3,0,2,1:T(8,128)S(1)} collective-permute-done((f32[8,8,6,1]{3,0,2,1:T(8,128)S(1)}, f32[8,8,6,1]{3,0,2,1:T(8,128)S(1)}, u32[]{:S(2)}, u32[]{:S(2)}) %collective-permute-start.2) | collective-permute-done | bytes 1568 | tf_op jit(solution)/shard_map/while/body/eval_jaxpr/ppermute | solution.py:20
  310.1 4.9 %collective-permute-done.3 = f32[8,8,6,1]{3,0,2,1:T(8,128)S(1)} collective-permute-done((f32[8,8,6,1]{3,0,2,1:T(8,128)S(1)}, f32[8,8,6,1]{3,0,2,1:T(8,128)S(1)}, u32[]{:S(2)}, u32[]{:S(2)}) %collective-permute-start.3) | collective-permute-done | bytes 1568 | tf_op jit(solution)/shard_map/while/body/eval_jaxpr/ppermute | solution.py:19
  320.0 2.6 convolution_bitcast_fusion.2
  322.6 39.1 %all-reduce.2 = (f32[]{:T(128)}, f32[6]{0:T(128)S(1)}, f32[]{:T(128)}) all-reduce(f32[]{:T(128)} %get-tuple-element.835, f32[6]{0:T(128)S(1)} %convolution_bitcast_fusion.2, f32[]{:T(128)} %fusion.189), channel_id=1, replica_groups=mesh['gx'=4,'gy'=8] {'gx','gy'}, use_global_device_ids=true, to_apply=%region_2.2 | all-reduce | flops 8 | bytes 64 | tf_op jit(solution)/shard_map/while/body/eval_jaxpr/psum | solution.py:108
  363.2 1.4 fusion.191
  364.7 0.8 multiply_reduce_fusion.4
  366.2 40.3 %psum.52 = f32[]{:T(128)} all-reduce(f32[]{:T(128)} %multiply_reduce_fusion.2), channel_id=1, replica_groups=mesh['gx'=4,'gy'=8] {'gx','gy'}, use_global_device_ids=true, to_apply=%region_8.9 | all-reduce | flops 1 | bytes 8 | tf_op jit(solution)/shard_map/psum | solution.py:74
  407.2 0.8 select_add_fusion.1
  (290 shorter events, 35.2 us)
Async XLA Ops:
  1.5 2.6 copy-start.5
  1.6 4.1 %collective-permute-start.4 = (f32[8,8,1,128]{3,0,2,1:T(8,128)S(1)}, f32[8,8,1,128]{3,0,2,1:T(8,128)S(1)}, u32[]{:S(2)}, u32[]{:S(2)}) collective-permute-start(f32[8,8,1,128]{3,0,2,1:T(8,128)S(1)} %copy.247), channel_id=1, source_target_pairs={{0,8},{8,16},{16,24},{24,0},{1,9},{9,17},{17,25},{25,1},{2,10},{10... | collective-permute-start | bytes 98312 | tf_op jit(solution)/shard_map/ppermute | solution.py:19
  2.1 2.1 copy-start.11
  2.1 2.1 copy-start.6
  2.2 3.7 collective-permute-start.5
  4.2 0.9 copy-start.7
  4.2 0.9 copy-start.9
  5.5 6.7 %copy-start.3 = (f32[8,8,4,128]{3,0,2,1:T(8,128)}, f32[8,8,4,128]{3,0,2,1:T(8,128)S(1)}, u32[]{:S(2)}) copy-start(f32[8,8,4,128]{3,0,2,1:T(8,128)S(1)} %fusion.62) | copy-start | bytes 393220
  6.0 11.1 %collective-permute-start.6 = (f32[8,8,6,1]{3,0,2,1:T(8,128)S(1)}, f32[8,8,6,1]{3,0,2,1:T(8,128)S(1)}, u32[]{:S(2)}, u32[]{:S(2)}) collective-permute-start(f32[8,8,6,1]{3,0,2,1:T(8,128)S(1)} %get-tuple-element.682), channel_id=1, source_target_pairs={{0,1},{1,2},{2,3},{3,4},{4,5},{5,6},{6,7},{7,0},{8,9},{9,10},{10,1... | collective-permute-start | bytes 4616 | tf_op jit(solution)/shard_map/ppermute | solution.py:19
  8.2 11.6 %collective-permute-start.7 = (f32[8,8,6,1]{3,0,2,1:T(8,128)S(1)}, f32[8,8,6,1]{3,0,2,1:T(8,128)S(1)}, u32[]{:S(2)}, u32[]{:S(2)}) collective-permute-start(f32[8,8,6,1]{3,0,2,1:T(8,128)S(1)} %get-tuple-element.683), channel_id=1, source_target_pairs={{1,0},{2,1},{3,2},{4,3},{5,4},{6,5},{7,6},{0,7},{9,8},{10,9},{11,1... | collective-permute-start | bytes 4616 | tf_op jit(solution)/shard_map/ppermute | solution.py:20
  11.4 0.7 copy-start.10
  22.5 0.7 slice-start.1
  22.6 0.9 copy-start.4
  24.1 0.9 copy-start.8
  26.1 3.4 collective-permute-start
  26.3 3.2 collective-permute-start.1
  28.5 4.2 %copy-start.1 = (f32[8,8,4,128]{3,0,2,1:T(8,128)}, f32[8,8,4,128]{3,0,2,1:T(8,128)S(1)}, u32[]{:S(2)}) copy-start(f32[8,8,4,128]{3,0,2,1:T(8,128)S(1)} %fusion.175) | copy-start | bytes 393220 | tf_op jit(solution)/shard_map/while
  29.6 7.4 %collective-permute-start.2 = (f32[8,8,6,1]{3,0,2,1:T(8,128)S(1)}, f32[8,8,6,1]{3,0,2,1:T(8,128)S(1)}, u32[]{:S(2)}, u32[]{:S(2)}) collective-permute-start(f32[8,8,6,1]{3,0,2,1:T(8,128)S(1)} %get-tuple-element.788), channel_id=1, source_target_pairs={{1,0},{2,1},{3,2},{4,3},{5,4},{6,5},{7,6},{0,7},{9,8},{10,9},{11,1... | collective-permute-start | bytes 4616 | tf_op jit(solution)/shard_map/while/body/eval_jaxpr/ppermute | solution.py:20
  32.4 9.8 %collective-permute-start.3 = (f32[8,8,6,1]{3,0,2,1:T(8,128)S(1)}, f32[8,8,6,1]{3,0,2,1:T(8,128)S(1)}, u32[]{:S(2)}, u32[]{:S(2)}) collective-permute-start(f32[8,8,6,1]{3,0,2,1:T(8,128)S(1)} %get-tuple-element.789), channel_id=1, source_target_pairs={{0,1},{1,2},{2,3},{3,4},{4,5},{5,6},{6,7},{7,0},{8,9},{9,10},{10,1... | collective-permute-start | bytes 4616 | tf_op jit(solution)/shard_map/while/body/eval_jaxpr/ppermute | solution.py:19
  44.9 0.7 slice-start
  45.0 0.9 copy-start.2
  93.1 3.4 collective-permute-start
  93.2 3.5 collective-permute-start.1
  95.5 5.4 %copy-start.1 = (f32[8,8,4,128]{3,0,2,1:T(8,128)}, f32[8,8,4,128]{3,0,2,1:T(8,128)S(1)}, u32[]{:S(2)}) copy-start(f32[8,8,4,128]{3,0,2,1:T(8,128)S(1)} %fusion.175) | copy-start | bytes 393220 | tf_op jit(solution)/shard_map/while
  96.8 9.2 %collective-permute-start.2 = (f32[8,8,6,1]{3,0,2,1:T(8,128)S(1)}, f32[8,8,6,1]{3,0,2,1:T(8,128)S(1)}, u32[]{:S(2)}, u32[]{:S(2)}) collective-permute-start(f32[8,8,6,1]{3,0,2,1:T(8,128)S(1)} %get-tuple-element.788), channel_id=1, source_target_pairs={{1,0},{2,1},{3,2},{4,3},{5,4},{6,5},{7,6},{0,7},{9,8},{10,9},{11,1... | collective-permute-start | bytes 4616 | tf_op jit(solution)/shard_map/while/body/eval_jaxpr/ppermute | solution.py:20
  100.7 10.3 %collective-permute-start.3 = (f32[8,8,6,1]{3,0,2,1:T(8,128)S(1)}, f32[8,8,6,1]{3,0,2,1:T(8,128)S(1)}, u32[]{:S(2)}, u32[]{:S(2)}) collective-permute-start(f32[8,8,6,1]{3,0,2,1:T(8,128)S(1)} %get-tuple-element.789), channel_id=1, source_target_pairs={{0,1},{1,2},{2,3},{3,4},{4,5},{5,6},{6,7},{7,0},{8,9},{9,10},{10,1... | collective-permute-start | bytes 4616 | tf_op jit(solution)/shard_map/while/body/eval_jaxpr/ppermute | solution.py:19
  113.6 0.7 slice-start
  113.8 0.9 copy-start.2
  161.7 3.4 collective-permute-start
  161.8 3.5 collective-permute-start.1
  164.1 5.4 %copy-start.1 = (f32[8,8,4,128]{3,0,2,1:T(8,128)}, f32[8,8,4,128]{3,0,2,1:T(8,128)S(1)}, u32[]{:S(2)}) copy-start(f32[8,8,4,128]{3,0,2,1:T(8,128)S(1)} %fusion.175) | copy-start | bytes 393220 | tf_op jit(solution)/shard_map/while
  165.4 8.8 %collective-permute-start.2 = (f32[8,8,6,1]{3,0,2,1:T(8,128)S(1)}, f32[8,8,6,1]{3,0,2,1:T(8,128)S(1)}, u32[]{:S(2)}, u32[]{:S(2)}) collective-permute-start(f32[8,8,6,1]{3,0,2,1:T(8,128)S(1)} %get-tuple-element.788), channel_id=1, source_target_pairs={{1,0},{2,1},{3,2},{4,3},{5,4},{6,5},{7,6},{0,7},{9,8},{10,9},{11,1... | collective-permute-start | bytes 4616 | tf_op jit(solution)/shard_map/while/body/eval_jaxpr/ppermute | solution.py:20
  169.3 9.8 %collective-permute-start.3 = (f32[8,8,6,1]{3,0,2,1:T(8,128)S(1)}, f32[8,8,6,1]{3,0,2,1:T(8,128)S(1)}, u32[]{:S(2)}, u32[]{:S(2)}) collective-permute-start(f32[8,8,6,1]{3,0,2,1:T(8,128)S(1)} %get-tuple-element.789), channel_id=1, source_target_pairs={{0,1},{1,2},{2,3},{3,4},{4,5},{5,6},{6,7},{7,0},{8,9},{9,10},{10,1... | collective-permute-start | bytes 4616 | tf_op jit(solution)/shard_map/while/body/eval_jaxpr/ppermute | solution.py:19
  181.8 0.7 slice-start
  181.9 0.9 copy-start.2
  229.7 3.4 collective-permute-start
  229.7 3.5 collective-permute-start.1
  232.1 5.4 %copy-start.1 = (f32[8,8,4,128]{3,0,2,1:T(8,128)}, f32[8,8,4,128]{3,0,2,1:T(8,128)S(1)}, u32[]{:S(2)}) copy-start(f32[8,8,4,128]{3,0,2,1:T(8,128)S(1)} %fusion.175) | copy-start | bytes 393220 | tf_op jit(solution)/shard_map/while
  233.3 8.8 %collective-permute-start.2 = (f32[8,8,6,1]{3,0,2,1:T(8,128)S(1)}, f32[8,8,6,1]{3,0,2,1:T(8,128)S(1)}, u32[]{:S(2)}, u32[]{:S(2)}) collective-permute-start(f32[8,8,6,1]{3,0,2,1:T(8,128)S(1)} %get-tuple-element.788), channel_id=1, source_target_pairs={{1,0},{2,1},{3,2},{4,3},{5,4},{6,5},{7,6},{0,7},{9,8},{10,9},{11,1... | collective-permute-start | bytes 4616 | tf_op jit(solution)/shard_map/while/body/eval_jaxpr/ppermute | solution.py:20
  237.3 9.8 %collective-permute-start.3 = (f32[8,8,6,1]{3,0,2,1:T(8,128)S(1)}, f32[8,8,6,1]{3,0,2,1:T(8,128)S(1)}, u32[]{:S(2)}, u32[]{:S(2)}) collective-permute-start(f32[8,8,6,1]{3,0,2,1:T(8,128)S(1)} %get-tuple-element.789), channel_id=1, source_target_pairs={{0,1},{1,2},{2,3},{3,4},{4,5},{5,6},{6,7},{7,0},{8,9},{9,10},{10,1... | collective-permute-start | bytes 4616 | tf_op jit(solution)/shard_map/while/body/eval_jaxpr/ppermute | solution.py:19
  249.7 0.7 slice-start
  249.9 0.9 copy-start.2
  297.6 3.4 collective-permute-start
  297.7 3.5 collective-permute-start.1
  300.0 5.4 %copy-start.1 = (f32[8,8,4,128]{3,0,2,1:T(8,128)}, f32[8,8,4,128]{3,0,2,1:T(8,128)S(1)}, u32[]{:S(2)}) copy-start(f32[8,8,4,128]{3,0,2,1:T(8,128)S(1)} %fusion.175) | copy-start | bytes 393220 | tf_op jit(solution)/shard_map/while
  301.3 8.8 %collective-permute-start.2 = (f32[8,8,6,1]{3,0,2,1:T(8,128)S(1)}, f32[8,8,6,1]{3,0,2,1:T(8,128)S(1)}, u32[]{:S(2)}, u32[]{:S(2)}) collective-permute-start(f32[8,8,6,1]{3,0,2,1:T(8,128)S(1)} %get-tuple-element.788), channel_id=1, source_target_pairs={{1,0},{2,1},{3,2},{4,3},{5,4},{6,5},{7,6},{0,7},{9,8},{10,9},{11,1... | collective-permute-start | bytes 4616 | tf_op jit(solution)/shard_map/while/body/eval_jaxpr/ppermute | solution.py:20
  305.2 9.8 %collective-permute-start.3 = (f32[8,8,6,1]{3,0,2,1:T(8,128)S(1)}, f32[8,8,6,1]{3,0,2,1:T(8,128)S(1)}, u32[]{:S(2)}, u32[]{:S(2)}) collective-permute-start(f32[8,8,6,1]{3,0,2,1:T(8,128)S(1)} %get-tuple-element.789), channel_id=1, source_target_pairs={{0,1},{1,2},{2,3},{3,4},{4,5},{5,6},{6,7},{7,0},{8,9},{9,10},{10,1... | collective-permute-start | bytes 4616 | tf_op jit(solution)/shard_map/while/body/eval_jaxpr/ppermute | solution.py:19
  317.7 0.7 slice-start
  317.8 0.9 copy-start.2
  407.2 0.9 copy-start
where the time goes:
time: 410 us; the launch traced here: 408 us
  blocking collectives  236 us (58%)
  waiting for transfers between devices  61.2 us (15%)
  matrix products  36.9 us (9%)
  starting transfers between devices  35.6 us (9%)
  local copies, waits for them, and re-layouts  15.6 us (4%)
  other arithmetic  13.3 us (3%)
  loops' own time  7.86 us (2%)
    psum x5, blocking collectives, advance(): lax.psum((local, local_total(pending * image), local_total(pending * pend...  196 us
    psum x1, blocking collectives, norm_scale(): squares = lax.psum(local_total(vector * vector), ('gx', 'gy'))  40.3 us
    ppermute x12, waiting for transfers between devices, extended(): before = lax.ppermute(last, axis, up)  34.7 us
    ppermute x12, starting transfers between devices, extended(): after = lax.ppermute(leading, axis, down)  32.4 us
    ppermute x12, waiting for transfers between devices, extended(): after = lax.ppermute(leading, axis, down)  26.5 us
    dot_general x5, matrix products, products(): per_cell = jnp.einsum('kqxy,qxy->kxy', basis, image, precision=highest)  13 us
    reduce_sum x12, other arithmetic, local_total(): return jnp.sum(jnp.sum(values, axis=0))  8.74 us
  transfers between devices with their start and end apart: 24, of which 23 were waited for; matrix products, arithmetic and copies ran while one was open for 1% of the time, Pallas kernels for 0%

commit v1 on v0

--- a/solution.py
+++ b/solution.py
@@ -106,7 +106,8 @@
         image = operate(pending)
         local = products(basis, image)
         projected, crossed, squares = lax.psum(
-            (local, local_total(pending * image), local_total(pending * pending)), ("gx", "gy")
+            lax.psum((local, local_total(pending * image), local_total(pending * pending)), "gy"),
+            "gx",
         )
         beta = jnp.sqrt(squares / total + FLOOR)
         basis = lax.dynamic_update_index_in_dim(basis, pending / beta, step, 0)

time: 410 us -> 332 us (0.81)
  blocking collectives: 236 us -> 167 us
  starting transfers between devices: 35.6 us -> 28.2 us
    psum x5, blocking collectives: 196 us -> 98.4 us  [advance(): lax.psum((local, local_total(pending * image), local_total(pending * pend...]
    psum x0 -> x5, blocking collectives: none -> 31.7 us  [advance(): lax.psum(lax.psum((local, local_total(pending * image), local_total(pendi...]
    ppermute x12, waiting for transfers between devices: 34.7 us -> 19.4 us  [extended(): before = lax.ppermute(last, axis, up)]
    ppermute x12, waiting for transfers between devices: 26.5 us -> 41 us  [extended(): after = lax.ppermute(leading, axis, down)]
    ppermute x12, starting transfers between devices: 32.4 us -> 19.5 us  [extended(): after = lax.ppermute(leading, axis, down)]
    ppermute x12, starting transfers between devices: 3.28 us -> 8.7 us  [extended(): before = lax.ppermute(last, axis, up)]
  transfers between devices with their start and end apart: 24 -> 24, of which waited for: 23 -> 16; matrix products, arithmetic and copies ran while one was open for 1% -> 2% of each run, Pallas kernels for 0% -> 0%
where the time goes in v1:
time: 332 us; the launch traced here: 331 us
  blocking collectives  167 us (50%)
  waiting for transfers between devices  60.4 us (18%)
  matrix products  37 us (11%)
  starting transfers between devices  28.2 us (8%)
  local copies, waits for them, and re-layouts  15.6 us (5%)
  other arithmetic  13.2 us (4%)
  loops' own time  7.86 us (2%)
    psum x5, blocking collectives, advance(): lax.psum((local, local_total(pending * image), local_total(pending * pend...  98.4 us
    ppermute x12, waiting for transfers between devices, extended(): after = lax.ppermute(leading, axis, down)  41 us
    psum x1, blocking collectives, norm_scale(): squares = lax.psum(local_total(vector * vector), ('gx', 'gy'))  37 us
    psum x5, blocking collectives, advance(): lax.psum(lax.psum((local, local_total(pending * image), local_total(pendi...  31.7 us
    ppermute x12, starting transfers between devices, extended(): after = lax.ppermute(leading, axis, down)  19.5 us
    ppermute x12, waiting for transfers between devices, extended(): before = lax.ppermute(last, axis, up)  19.4 us
    dot_general x5, matrix products, products(): per_cell = jnp.einsum('kqxy,qxy->kxy', basis, image, precision=highest)  13 us
    ppermute x12, starting transfers between devices, extended(): before = lax.ppermute(last, axis, up)  8.7 us
  transfers between devices with their start and end apart: 24, of which 16 were waited for; matrix products, arithmetic and copies ran while one was open for 2% of the time, Pallas kernels for 0%

profile of v1, /device:TPU:0, one launch (start us, length us, event | category | flops | bytes accessed | tf_op | source)
XLA Modules:
  0.0 330.9 jit_solution(3461295096444661622)
XLA Ops:
  0.6 0.9 copy.257
  2.2 2.0 collective-permute-start.5
  6.0 2.2 collective-permute-start.6
  8.2 3.1 collective-permute-start.7
  12.3 4.8 %collective-permute-done.6 = f32[8,8,6,1]{3,0,2,1:T(8,128)S(1)} collective-permute-done((f32[8,8,6,1]{3,0,2,1:T(8,128)S(1)}, f32[8,8,6,1]{3,0,2,1:T(8,128)S(1)}, u32[]{:S(2)}, u32[]{:S(2)}) %collective-permute-start.6) | collective-permute-done | bytes 1568 | tf_op jit(solution)/shard_map/ppermute | solution.py:19
  17.1 2.8 collective-permute-done.7
  20.9 0.7 fusion.63
  24.3 0.7 copy-done.8
  25.1 0.8 multiply_reduce_fusion.1
  26.0 265.6 %while.31 = (s32[]{:T(128)}, f32[6,64,4,128]{3,2,1,0:T(4,128)S(1)}, f32[6,5]{1,0:T(8,128)S(1)}, f32[64,4,128]{2,1,0:T(4,128)S(1)}, f32[64,4,128]{2,0,1:T(8,128)S...) while((s32[]{:T(128)}, f32[6,64,4,128]{3,2,1,0:T(4,128)S(1)}, ...), condition=%wide.region_9.10_spmd.clone.clone, body=%wide.region_0.9_spmd.clone.clone.sunk | while | flops 14006077 | bytes 9489099 | solution.py:122
  26.3 1.6 collective-permute-start.1
  28.5 1.0 collective-permute-done
  29.6 2.8 collective-permute-start.2
  32.7 4.3 %collective-permute-done.2 = f32[8,8,6,1]{3,0,2,1:T(8,128)S(1)} collective-permute-done((f32[8,8,6,1]{3,0,2,1:T(8,128)S(1)}, f32[8,8,6,1]{3,0,2,1:T(8,128)S(1)}, u32[]{:S(2)}, u32[]{:S(2)}) %collective-permute-start.2) | collective-permute-done | bytes 1568 | tf_op jit(solution)/shard_map/while/body/eval_jaxpr/ppermute | solution.py:20
  37.0 5.2 %collective-permute-done.3 = f32[8,8,6,1]{3,0,2,1:T(8,128)S(1)} collective-permute-done((f32[8,8,6,1]{3,0,2,1:T(8,128)S(1)}, f32[8,8,6,1]{3,0,2,1:T(8,128)S(1)}, u32[]{:S(2)}, u32[]{:S(2)}) %collective-permute-start.3) | collective-permute-done | bytes 1568 | tf_op jit(solution)/shard_map/while/body/eval_jaxpr/ppermute | solution.py:19
  43.1 0.7 fusion.184
  47.2 2.6 convolution_bitcast_fusion.2
  49.8 22.0 %all-reduce.4 = (f32[]{:T(128)}, f32[6]{0:T(128)S(1)}, f32[]{:T(128)}) all-reduce(f32[]{:T(128)} %get-tuple-element.844, f32[6]{0:T(128)S(1)} %convolution_bitcast_fusion.2, f32[]{:T(128)} %fusion.189), channel_id=1, replica_groups=mesh['gx'=4,'gy'=8] {'gy'}, use_global_device_ids=true, to_apply=%region_2.2 | all-reduce | flops 8 | bytes 64 | tf_op jit(solution)/shard_map/while/body/eval_jaxpr/psum | solution.py:109
  71.8 6.3 %all-reduce.5 = (f32[]{:T(128)}, f32[6]{0:T(128)S(1)}, f32[]{:T(128)}) all-reduce(f32[]{:T(128)} %get-tuple-element.810, f32[6]{0:T(128)S(1)} %get-tuple-element.811, f32[]{:T(128)} %get-tuple-element.812), channel_id=1, replica_groups=mesh['gx'=4,'gy'=8] {'gx'}, use_global_device_ids=true, to_apply=%region_3.3 | all-reduce | flops 8 | bytes 64 | tf_op jit(solution)/shard_map/while/body/eval_jaxpr/psum | solution.py:108
  79.6 1.4 fusion.191
  81.1 0.8 multiply_reduce_fusion.4
  82.1 1.8 collective-permute-start.1
  84.5 1.0 collective-permute-done
  85.7 2.0 collective-permute-start.3
  87.9 9.6 %collective-permute-done.2 = f32[8,8,6,1]{3,0,2,1:T(8,128)S(1)} collective-permute-done((f32[8,8,6,1]{3,0,2,1:T(8,128)S(1)}, f32[8,8,6,1]{3,0,2,1:T(8,128)S(1)}, u32[]{:S(2)}, u32[]{:S(2)}) %collective-permute-start.2) | collective-permute-done | bytes 1568 | tf_op jit(solution)/shard_map/while/body/eval_jaxpr/ppermute | solution.py:20
  98.4 0.7 fusion.184
  102.6 2.6 convolution_bitcast_fusion.2
  105.2 18.0 %all-reduce.4 = (f32[]{:T(128)}, f32[6]{0:T(128)S(1)}, f32[]{:T(128)}) all-reduce(f32[]{:T(128)} %get-tuple-element.844, f32[6]{0:T(128)S(1)} %convolution_bitcast_fusion.2, f32[]{:T(128)} %fusion.189), channel_id=1, replica_groups=mesh['gx'=4,'gy'=8] {'gy'}, use_global_device_ids=true, to_apply=%region_2.2 | all-reduce | flops 8 | bytes 64 | tf_op jit(solution)/shard_map/while/body/eval_jaxpr/psum | solution.py:109
  123.1 6.3 %all-reduce.5 = (f32[]{:T(128)}, f32[6]{0:T(128)S(1)}, f32[]{:T(128)}) all-reduce(f32[]{:T(128)} %get-tuple-element.810, f32[6]{0:T(128)S(1)} %get-tuple-element.811, f32[]{:T(128)} %get-tuple-element.812), channel_id=1, replica_groups=mesh['gx'=4,'gy'=8] {'gx'}, use_global_device_ids=true, to_apply=%region_3.3 | all-reduce | flops 8 | bytes 64 | tf_op jit(solution)/shard_map/while/body/eval_jaxpr/psum | solution.py:108
  130.9 1.4 fusion.191
  132.5 0.8 multiply_reduce_fusion.4
  133.4 1.8 collective-permute-start.1
  135.8 1.0 collective-permute-done
  136.9 1.9 collective-permute-start.2
  139.3 5.3 %collective-permute-done.2 = f32[8,8,6,1]{3,0,2,1:T(8,128)S(1)} collective-permute-done((f32[8,8,6,1]{3,0,2,1:T(8,128)S(1)}, f32[8,8,6,1]{3,0,2,1:T(8,128)S(1)}, u32[]{:S(2)}, u32[]{:S(2)}) %collective-permute-start.2) | collective-permute-done | bytes 1568 | tf_op jit(solution)/shard_map/while/body/eval_jaxpr/ppermute | solution.py:20
  144.5 4.5 %collective-permute-done.3 = f32[8,8,6,1]{3,0,2,1:T(8,128)S(1)} collective-permute-done((f32[8,8,6,1]{3,0,2,1:T(8,128)S(1)}, f32[8,8,6,1]{3,0,2,1:T(8,128)S(1)}, u32[]{:S(2)}, u32[]{:S(2)}) %collective-permute-start.3) | collective-permute-done | bytes 1568 | tf_op jit(solution)/shard_map/while/body/eval_jaxpr/ppermute | solution.py:19
  149.9 0.7 fusion.184
  154.1 2.6 convolution_bitcast_fusion.2
  156.6 19.7 %all-reduce.4 = (f32[]{:T(128)}, f32[6]{0:T(128)S(1)}, f32[]{:T(128)}) all-reduce(f32[]{:T(128)} %get-tuple-element.844, f32[6]{0:T(128)S(1)} %convolution_bitcast_fusion.2, f32[]{:T(128)} %fusion.189), channel_id=1, replica_groups=mesh['gx'=4,'gy'=8] {'gy'}, use_global_device_ids=true, to_apply=%region_2.2 | all-reduce | flops 8 | bytes 64 | tf_op jit(solution)/shard_map/while/body/eval_jaxpr/psum | solution.py:109
  176.3 6.3 %all-reduce.5 = (f32[]{:T(128)}, f32[6]{0:T(128)S(1)}, f32[]{:T(128)}) all-reduce(f32[]{:T(128)} %get-tuple-element.810, f32[6]{0:T(128)S(1)} %get-tuple-element.811, f32[]{:T(128)} %get-tuple-element.812), channel_id=1, replica_groups=mesh['gx'=4,'gy'=8] {'gx'}, use_global_device_ids=true, to_apply=%region_3.3 | all-reduce | flops 8 | bytes 64 | tf_op jit(solution)/shard_map/while/body/eval_jaxpr/psum | solution.py:108
  184.1 1.4 fusion.191
  185.6 0.8 multiply_reduce_fusion.4
  186.6 1.8 collective-permute-start.1
  188.9 1.0 collective-permute-done
  190.3 1.9 collective-permute-start.3
  192.4 9.4 %collective-permute-done.2 = f32[8,8,6,1]{3,0,2,1:T(8,128)S(1)} collective-permute-done((f32[8,8,6,1]{3,0,2,1:T(8,128)S(1)}, f32[8,8,6,1]{3,0,2,1:T(8,128)S(1)}, u32[]{:S(2)}, u32[]{:S(2)}) %collective-permute-start.2) | collective-permute-done | bytes 1568 | tf_op jit(solution)/shard_map/while/body/eval_jaxpr/ppermute | solution.py:20
  206.9 2.6 convolution_bitcast_fusion.2
  209.5 19.1 %all-reduce.4 = (f32[]{:T(128)}, f32[6]{0:T(128)S(1)}, f32[]{:T(128)}) all-reduce(f32[]{:T(128)} %get-tuple-element.844, f32[6]{0:T(128)S(1)} %convolution_bitcast_fusion.2, f32[]{:T(128)} %fusion.189), channel_id=1, replica_groups=mesh['gx'=4,'gy'=8] {'gy'}, use_global_device_ids=true, to_apply=%region_2.2 | all-reduce | flops 8 | bytes 64 | tf_op jit(solution)/shard_map/while/body/eval_jaxpr/psum | solution.py:109
  228.6 6.3 %all-reduce.5 = (f32[]{:T(128)}, f32[6]{0:T(128)S(1)}, f32[]{:T(128)}) all-reduce(f32[]{:T(128)} %get-tuple-element.810, f32[6]{0:T(128)S(1)} %get-tuple-element.811, f32[]{:T(128)} %get-tuple-element.812), channel_id=1, replica_groups=mesh['gx'=4,'gy'=8] {'gx'}, use_global_device_ids=true, to_apply=%region_3.3 | all-reduce | flops 8 | bytes 64 | tf_op jit(solution)/shard_map/while/body/eval_jaxpr/psum | solution.py:108
  236.4 1.4 fusion.191
  237.9 0.8 multiply_reduce_fusion.4
  238.9 1.8 collective-permute-start.1
  241.2 1.0 collective-permute-done
  242.4 0.7 collective-permute-start.2
  243.1 1.4 collective-permute-start.3
  244.7 9.4 %collective-permute-done.2 = f32[8,8,6,1]{3,0,2,1:T(8,128)S(1)} collective-permute-done((f32[8,8,6,1]{3,0,2,1:T(8,128)S(1)}, f32[8,8,6,1]{3,0,2,1:T(8,128)S(1)}, u32[]{:S(2)}, u32[]{:S(2)}) %collective-permute-start.2) | collective-permute-done | bytes 1568 | tf_op jit(solution)/shard_map/while/body/eval_jaxpr/ppermute | solution.py:20
  254.3 0.7 fusion.185
  259.1 2.6 convolution_bitcast_fusion.2
  261.7 19.6 %all-reduce.4 = (f32[]{:T(128)}, f32[6]{0:T(128)S(1)}, f32[]{:T(128)}) all-reduce(f32[]{:T(128)} %get-tuple-element.844, f32[6]{0:T(128)S(1)} %convolution_bitcast_fusion.2, f32[]{:T(128)} %fusion.189), channel_id=1, replica_groups=mesh['gx'=4,'gy'=8] {'gy'}, use_global_device_ids=true, to_apply=%region_2.2 | all-reduce | flops 8 | bytes 64 | tf_op jit(solution)/shard_map/while/body/eval_jaxpr/psum | solution.py:109
  281.4 6.3 %all-reduce.5 = (f32[]{:T(128)}, f32[6]{0:T(128)S(1)}, f32[]{:T(128)}) all-reduce(f32[]{:T(128)} %get-tuple-element.810, f32[6]{0:T(128)S(1)} %get-tuple-element.811, f32[]{:T(128)} %get-tuple-element.812), channel_id=1, replica_groups=mesh['gx'=4,'gy'=8] {'gx'}, use_global_device_ids=true, to_apply=%region_3.3 | all-reduce | flops 8 | bytes 64 | tf_op jit(solution)/shard_map/while/body/eval_jaxpr/psum | solution.py:108
  289.2 1.4 fusion.191
  290.7 0.8 multiply_reduce_fusion.4
  292.2 37.0 %psum.97 = f32[]{:T(128)} all-reduce(f32[]{:T(128)} %multiply_reduce_fusion.2), channel_id=1, replica_groups=mesh['gx'=4,'gy'=8] {'gx','gy'}, use_global_device_ids=true, to_apply=%region_11.12 | all-reduce | flops 1 | bytes 8 | tf_op jit(solution)/shard_map/psum | solution.py:74
  330.0 0.8 select_add_fusion.1
  (295 shorter events, 37.3 us)
Async XLA Ops:
  1.5 2.6 copy-start.5
  1.6 4.1 %collective-permute-start.4 = (f32[8,8,1,128]{3,0,2,1:T(8,128)S(1)}, f32[8,8,1,128]{3,0,2,1:T(8,128)S(1)}, u32[]{:S(2)}, u32[]{:S(2)}) collective-permute-start(f32[8,8,1,128]{3,0,2,1:T(8,128)S(1)} %copy.247), channel_id=1, source_target_pairs={{0,8},{8,16},{16,24},{24,0},{1,9},{9,17},{17,25},{25,1},{2,10},{10... | collective-permute-start | bytes 98312 | tf_op jit(solution)/shard_map/ppermute | solution.py:19
  2.1 2.1 copy-start.11
  2.1 2.1 copy-start.6
  2.2 3.7 %collective-permute-start.5 = (f32[8,8,1,128]{3,0,2,1:T(8,128)S(1)}, f32[8,8,1,128]{3,0,2,1:T(8,128)S(1)}, u32[]{:S(2)}, u32[]{:S(2)}) collective-permute-start(f32[8,8,1,128]{3,0,2,1:T(8,128)S(1)} %copy.248), channel_id=1, source_target_pairs={{8,0},{16,8},{24,16},{0,24},{9,1},{17,9},{25,17},{1,25},{10,2},{18... | collective-permute-start | bytes 98312 | tf_op jit(solution)/shard_map/ppermute | solution.py:20
  4.2 0.9 copy-start.7
  4.2 0.9 copy-start.9
  5.5 6.7 %copy-start.3 = (f32[8,8,4,128]{3,0,2,1:T(8,128)}, f32[8,8,4,128]{3,0,2,1:T(8,128)S(1)}, u32[]{:S(2)}) copy-start(f32[8,8,4,128]{3,0,2,1:T(8,128)S(1)} %fusion.62) | copy-start | bytes 393220
  6.0 11.1 %collective-permute-start.6 = (f32[8,8,6,1]{3,0,2,1:T(8,128)S(1)}, f32[8,8,6,1]{3,0,2,1:T(8,128)S(1)}, u32[]{:S(2)}, u32[]{:S(2)}) collective-permute-start(f32[8,8,6,1]{3,0,2,1:T(8,128)S(1)} %get-tuple-element.685), channel_id=1, source_target_pairs={{0,1},{1,2},{2,3},{3,4},{4,5},{5,6},{6,7},{7,0},{8,9},{9,10},{10,1... | collective-permute-start | bytes 4616 | tf_op jit(solution)/shard_map/ppermute | solution.py:19
  8.2 11.6 %collective-permute-start.7 = (f32[8,8,6,1]{3,0,2,1:T(8,128)S(1)}, f32[8,8,6,1]{3,0,2,1:T(8,128)S(1)}, u32[]{:S(2)}, u32[]{:S(2)}) collective-permute-start(f32[8,8,6,1]{3,0,2,1:T(8,128)S(1)} %get-tuple-element.686), channel_id=1, source_target_pairs={{1,0},{2,1},{3,2},{4,3},{5,4},{6,5},{7,6},{0,7},{9,8},{10,9},{11,1... | collective-permute-start | bytes 4616 | tf_op jit(solution)/shard_map/ppermute | solution.py:20
  11.4 0.7 copy-start.10
  22.5 0.7 slice-start.1
  22.6 0.9 copy-start.4
  24.1 0.9 copy-start.8
  26.0 3.4 %collective-permute-start = (f32[8,8,1,128]{3,0,2,1:T(8,128)S(1)}, f32[8,8,1,128]{3,0,2,1:T(8,128)S(1)}, u32[]{:S(2)}, u32[]{:S(2)}) collective-permute-start(f32[8,8,1,128]{3,0,2,1:T(8,128)S(1)} %copy.311), channel_id=1, source_target_pairs={{0,8},{8,16},{16,24},{24,0},{1,9},{9,17},{17,25},{25,1},{2,10},{10... | collective-permute-start | bytes 98312 | tf_op jit(solution)/shard_map/while/body/eval_jaxpr/ppermute | solution.py:19
  26.3 3.2 collective-permute-start.1
  28.5 4.2 %copy-start.1 = (f32[8,8,4,128]{3,0,2,1:T(8,128)}, f32[8,8,4,128]{3,0,2,1:T(8,128)S(1)}, u32[]{:S(2)}) copy-start(f32[8,8,4,128]{3,0,2,1:T(8,128)S(1)} %fusion.175) | copy-start | bytes 393220 | tf_op jit(solution)/shard_map/while
  29.6 7.4 %collective-permute-start.2 = (f32[8,8,6,1]{3,0,2,1:T(8,128)S(1)}, f32[8,8,6,1]{3,0,2,1:T(8,128)S(1)}, u32[]{:S(2)}, u32[]{:S(2)}) collective-permute-start(f32[8,8,6,1]{3,0,2,1:T(8,128)S(1)} %get-tuple-element.794), channel_id=1, source_target_pairs={{1,0},{2,1},{3,2},{4,3},{5,4},{6,5},{7,6},{0,7},{9,8},{10,9},{11,1... | collective-permute-start | bytes 4616 | tf_op jit(solution)/shard_map/while/body/eval_jaxpr/ppermute | solution.py:20
  32.4 9.8 %collective-permute-start.3 = (f32[8,8,6,1]{3,0,2,1:T(8,128)S(1)}, f32[8,8,6,1]{3,0,2,1:T(8,128)S(1)}, u32[]{:S(2)}, u32[]{:S(2)}) collective-permute-start(f32[8,8,6,1]{3,0,2,1:T(8,128)S(1)} %get-tuple-element.795), channel_id=1, source_target_pairs={{0,1},{1,2},{2,3},{3,4},{4,5},{5,6},{6,7},{7,0},{8,9},{9,10},{10,1... | collective-permute-start | bytes 4616 | tf_op jit(solution)/shard_map/while/body/eval_jaxpr/ppermute | solution.py:19
  44.9 0.7 slice-start
  45.0 0.9 copy-start.2
  82.0 3.4 %collective-permute-start = (f32[8,8,1,128]{3,0,2,1:T(8,128)S(1)}, f32[8,8,1,128]{3,0,2,1:T(8,128)S(1)}, u32[]{:S(2)}, u32[]{:S(2)}) collective-permute-start(f32[8,8,1,128]{3,0,2,1:T(8,128)S(1)} %copy.311), channel_id=1, source_target_pairs={{0,8},{8,16},{16,24},{24,0},{1,9},{9,17},{17,25},{25,1},{2,10},{10... | collective-permute-start | bytes 98312 | tf_op jit(solution)/shard_map/while/body/eval_jaxpr/ppermute | solution.py:19
  82.1 3.4 %collective-permute-start.1 = (f32[8,8,1,128]{3,0,2,1:T(8,128)S(1)}, f32[8,8,1,128]{3,0,2,1:T(8,128)S(1)}, u32[]{:S(2)}, u32[]{:S(2)}) collective-permute-start(f32[8,8,1,128]{3,0,2,1:T(8,128)S(1)} %copy.313), channel_id=1, source_target_pairs={{8,0},{16,8},{24,16},{0,24},{9,1},{17,9},{25,17},{1,25},{10,2},{18... | collective-permute-start | bytes 98312 | tf_op jit(solution)/shard_map/while/body/eval_jaxpr/ppermute | solution.py:20
  84.4 3.4 %copy-start.1 = (f32[8,8,4,128]{3,0,2,1:T(8,128)}, f32[8,8,4,128]{3,0,2,1:T(8,128)S(1)}, u32[]{:S(2)}) copy-start(f32[8,8,4,128]{3,0,2,1:T(8,128)S(1)} %fusion.175) | copy-start | bytes 393220 | tf_op jit(solution)/shard_map/while
  85.6 11.9 %collective-permute-start.2 = (f32[8,8,6,1]{3,0,2,1:T(8,128)S(1)}, f32[8,8,6,1]{3,0,2,1:T(8,128)S(1)}, u32[]{:S(2)}, u32[]{:S(2)}) collective-permute-start(f32[8,8,6,1]{3,0,2,1:T(8,128)S(1)} %get-tuple-element.794), channel_id=1, source_target_pairs={{1,0},{2,1},{3,2},{4,3},{5,4},{6,5},{7,6},{0,7},{9,8},{10,9},{11,1... | collective-permute-start | bytes 4616 | tf_op jit(solution)/shard_map/while/body/eval_jaxpr/ppermute | solution.py:20
  85.7 11.9 %collective-permute-start.3 = (f32[8,8,6,1]{3,0,2,1:T(8,128)S(1)}, f32[8,8,6,1]{3,0,2,1:T(8,128)S(1)}, u32[]{:S(2)}, u32[]{:S(2)}) collective-permute-start(f32[8,8,6,1]{3,0,2,1:T(8,128)S(1)} %get-tuple-element.795), channel_id=1, source_target_pairs={{0,1},{1,2},{2,3},{3,4},{4,5},{5,6},{6,7},{7,0},{8,9},{9,10},{10,1... | collective-permute-start | bytes 4616 | tf_op jit(solution)/shard_map/while/body/eval_jaxpr/ppermute | solution.py:19
  100.2 0.7 slice-start
  100.3 0.9 copy-start.2
  133.3 3.4 %collective-permute-start = (f32[8,8,1,128]{3,0,2,1:T(8,128)S(1)}, f32[8,8,1,128]{3,0,2,1:T(8,128)S(1)}, u32[]{:S(2)}, u32[]{:S(2)}) collective-permute-start(f32[8,8,1,128]{3,0,2,1:T(8,128)S(1)} %copy.311), channel_id=1, source_target_pairs={{0,8},{8,16},{16,24},{24,0},{1,9},{9,17},{17,25},{25,1},{2,10},{10... | collective-permute-start | bytes 98312 | tf_op jit(solution)/shard_map/while/body/eval_jaxpr/ppermute | solution.py:19
  133.4 3.4 %collective-permute-start.1 = (f32[8,8,1,128]{3,0,2,1:T(8,128)S(1)}, f32[8,8,1,128]{3,0,2,1:T(8,128)S(1)}, u32[]{:S(2)}, u32[]{:S(2)}) collective-permute-start(f32[8,8,1,128]{3,0,2,1:T(8,128)S(1)} %copy.313), channel_id=1, source_target_pairs={{8,0},{16,8},{24,16},{0,24},{9,1},{17,9},{25,17},{1,25},{10,2},{18... | collective-permute-start | bytes 98312 | tf_op jit(solution)/shard_map/while/body/eval_jaxpr/ppermute | solution.py:20
  135.8 3.4 %copy-start.1 = (f32[8,8,4,128]{3,0,2,1:T(8,128)}, f32[8,8,4,128]{3,0,2,1:T(8,128)S(1)}, u32[]{:S(2)}) copy-start(f32[8,8,4,128]{3,0,2,1:T(8,128)S(1)} %fusion.175) | copy-start | bytes 393220 | tf_op jit(solution)/shard_map/while
  136.9 7.6 %collective-permute-start.2 = (f32[8,8,6,1]{3,0,2,1:T(8,128)S(1)}, f32[8,8,6,1]{3,0,2,1:T(8,128)S(1)}, u32[]{:S(2)}, u32[]{:S(2)}) collective-permute-start(f32[8,8,6,1]{3,0,2,1:T(8,128)S(1)} %get-tuple-element.794), channel_id=1, source_target_pairs={{1,0},{2,1},{3,2},{4,3},{5,4},{6,5},{7,6},{0,7},{9,8},{10,9},{11,1... | collective-permute-start | bytes 4616 | tf_op jit(solution)/shard_map/while/body/eval_jaxpr/ppermute | solution.py:20
  138.8 10.2 %collective-permute-start.3 = (f32[8,8,6,1]{3,0,2,1:T(8,128)S(1)}, f32[8,8,6,1]{3,0,2,1:T(8,128)S(1)}, u32[]{:S(2)}, u32[]{:S(2)}) collective-permute-start(f32[8,8,6,1]{3,0,2,1:T(8,128)S(1)} %get-tuple-element.795), channel_id=1, source_target_pairs={{0,1},{1,2},{2,3},{3,4},{4,5},{5,6},{6,7},{7,0},{8,9},{9,10},{10,1... | collective-permute-start | bytes 4616 | tf_op jit(solution)/shard_map/while/body/eval_jaxpr/ppermute | solution.py:19
  151.7 0.7 slice-start
  151.8 0.9 copy-start.2
  186.5 3.4 %collective-permute-start = (f32[8,8,1,128]{3,0,2,1:T(8,128)S(1)}, f32[8,8,1,128]{3,0,2,1:T(8,128)S(1)}, u32[]{:S(2)}, u32[]{:S(2)}) collective-permute-start(f32[8,8,1,128]{3,0,2,1:T(8,128)S(1)} %copy.311), channel_id=1, source_target_pairs={{0,8},{8,16},{16,24},{24,0},{1,9},{9,17},{17,25},{25,1},{2,10},{10... | collective-permute-start | bytes 98312 | tf_op jit(solution)/shard_map/while/body/eval_jaxpr/ppermute | solution.py:19
  186.6 3.4 %collective-permute-start.1 = (f32[8,8,1,128]{3,0,2,1:T(8,128)S(1)}, f32[8,8,1,128]{3,0,2,1:T(8,128)S(1)}, u32[]{:S(2)}, u32[]{:S(2)}) collective-permute-start(f32[8,8,1,128]{3,0,2,1:T(8,128)S(1)} %copy.313), channel_id=1, source_target_pairs={{8,0},{16,8},{24,16},{0,24},{9,1},{17,9},{25,17},{1,25},{10,2},{18... | collective-permute-start | bytes 98312 | tf_op jit(solution)/shard_map/while/body/eval_jaxpr/ppermute | solution.py:20
  188.9 3.4 %copy-start.1 = (f32[8,8,4,128]{3,0,2,1:T(8,128)}, f32[8,8,4,128]{3,0,2,1:T(8,128)S(1)}, u32[]{:S(2)}) copy-start(f32[8,8,4,128]{3,0,2,1:T(8,128)S(1)} %fusion.175) | copy-start | bytes 393220 | tf_op jit(solution)/shard_map/while
  190.1 11.7 %collective-permute-start.2 = (f32[8,8,6,1]{3,0,2,1:T(8,128)S(1)}, f32[8,8,6,1]{3,0,2,1:T(8,128)S(1)}, u32[]{:S(2)}, u32[]{:S(2)}) collective-permute-start(f32[8,8,6,1]{3,0,2,1:T(8,128)S(1)} %get-tuple-element.794), channel_id=1, source_target_pairs={{1,0},{2,1},{3,2},{4,3},{5,4},{6,5},{7,6},{0,7},{9,8},{10,9},{11,1... | collective-permute-start | bytes 4616 | tf_op jit(solution)/shard_map/while/body/eval_jaxpr/ppermute | solution.py:20
  190.3 11.5 %collective-permute-start.3 = (f32[8,8,6,1]{3,0,2,1:T(8,128)S(1)}, f32[8,8,6,1]{3,0,2,1:T(8,128)S(1)}, u32[]{:S(2)}, u32[]{:S(2)}) collective-permute-start(f32[8,8,6,1]{3,0,2,1:T(8,128)S(1)} %get-tuple-element.795), channel_id=1, source_target_pairs={{0,1},{1,2},{2,3},{3,4},{4,5},{5,6},{6,7},{7,0},{8,9},{9,10},{10,1... | collective-permute-start | bytes 4616 | tf_op jit(solution)/shard_map/while/body/eval_jaxpr/ppermute | solution.py:19
  204.5 0.7 slice-start
  204.6 0.9 copy-start.2
  238.8 3.4 %collective-permute-start = (f32[8,8,1,128]{3,0,2,1:T(8,128)S(1)}, f32[8,8,1,128]{3,0,2,1:T(8,128)S(1)}, u32[]{:S(2)}, u32[]{:S(2)}) collective-permute-start(f32[8,8,1,128]{3,0,2,1:T(8,128)S(1)} %copy.311), channel_id=1, source_target_pairs={{0,8},{8,16},{16,24},{24,0},{1,9},{9,17},{17,25},{25,1},{2,10},{10... | collective-permute-start | bytes 98312 | tf_op jit(solution)/shard_map/while/body/eval_jaxpr/ppermute | solution.py:19
  238.9 3.4 %collective-permute-start.1 = (f32[8,8,1,128]{3,0,2,1:T(8,128)S(1)}, f32[8,8,1,128]{3,0,2,1:T(8,128)S(1)}, u32[]{:S(2)}, u32[]{:S(2)}) collective-permute-start(f32[8,8,1,128]{3,0,2,1:T(8,128)S(1)} %copy.313), channel_id=1, source_target_pairs={{8,0},{16,8},{24,16},{0,24},{9,1},{17,9},{25,17},{1,25},{10,2},{18... | collective-permute-start | bytes 98312 | tf_op jit(solution)/shard_map/while/body/eval_jaxpr/ppermute | solution.py:20
  241.2 3.4 %copy-start.1 = (f32[8,8,4,128]{3,0,2,1:T(8,128)}, f32[8,8,4,128]{3,0,2,1:T(8,128)S(1)}, u32[]{:S(2)}) copy-start(f32[8,8,4,128]{3,0,2,1:T(8,128)S(1)} %fusion.175) | copy-start | bytes 393220 | tf_op jit(solution)/shard_map/while
  242.4 11.7 %collective-permute-start.2 = (f32[8,8,6,1]{3,0,2,1:T(8,128)S(1)}, f32[8,8,6,1]{3,0,2,1:T(8,128)S(1)}, u32[]{:S(2)}, u32[]{:S(2)}) collective-permute-start(f32[8,8,6,1]{3,0,2,1:T(8,128)S(1)} %get-tuple-element.794), channel_id=1, source_target_pairs={{1,0},{2,1},{3,2},{4,3},{5,4},{6,5},{7,6},{0,7},{9,8},{10,9},{11,1... | collective-permute-start | bytes 4616 | tf_op jit(solution)/shard_map/while/body/eval_jaxpr/ppermute | solution.py:20
  243.1 11.0 %collective-permute-start.3 = (f32[8,8,6,1]{3,0,2,1:T(8,128)S(1)}, f32[8,8,6,1]{3,0,2,1:T(8,128)S(1)}, u32[]{:S(2)}, u32[]{:S(2)}) collective-permute-start(f32[8,8,6,1]{3,0,2,1:T(8,128)S(1)} %get-tuple-element.795), channel_id=1, source_target_pairs={{0,1},{1,2},{2,3},{3,4},{4,5},{5,6},{6,7},{7,0},{8,9},{9,10},{10,1... | collective-permute-start | bytes 4616 | tf_op jit(solution)/shard_map/while/body/eval_jaxpr/ppermute | solution.py:19
  256.8 0.7 slice-start
  256.9 0.9 copy-start.2
  330.0 0.9 copy-start
